TPU v7x, 32 devices: a whole 2x2x4 slice. The times are simulated.
32 devices in a mesh: row: 2 (over x), col: 4 (over y, core), depth: 4 (over z).
Axes of the slice: x: 2, y: 2, z: 4, core: 2. Of those that a mesh axis runs over, the one named last changes fastest.
Arguments:
- left_values: bfloat16 [96, 32, 4, 529], P('row', ('col', 'depth')), may hold values from -1.25 to 1.25
- left_columns: int32 [96, 32, 4], P('row', ('col', 'depth')), may hold values from 0 to 39, as said below
- right_values: bfloat16 [32, 40, 4, 3, 529], P(('col', 'depth'), 'row'), may hold values from -1.75 to 1.75
- right_columns: int32 [32, 40, 4, 3], P(('col', 'depth'), 'row'), may hold values from 0 to 31, as said below
Outputs:
- product_matrix: bfloat16 [2208, 2944], P('row', ('col', 'depth'))
Inputs may be any that keep to these rules, and one draw needn't show every extreme that they name: `left_columns`: within one block row and panel the 4 entries are distinct. `right_columns`: within one block row and column tile the 3 entries are distinct.
All inputs are finite; a program needn't handle non-finite values.
Results may differ from a plain program's by a relative error of at most 0.001.
Values may be sent and summed in bfloat16 or wider, within the bound.
A program may use at most 192 MiB of HBM per device.

v0:
```python
import math

import jax
import jax.numpy as jnp
from jax import lax
from jax.sharding import PartitionSpec as P

PANEL = 40
CTW = 32


def dense_left(values, columns, panel_width):
    rows_here, panels, slots, square = values.shape
    block_edge = math.isqrt(square)
    onehot = (
        columns.astype(jnp.float32)[..., None] == jnp.arange(panel_width, dtype=jnp.float32)
    ).astype(jnp.bfloat16)
    blocks = values.reshape(rows_here, panels, slots, block_edge, block_edge)
    filled = jnp.einsum(
        "mqsp,mqsab->qmapb", onehot, blocks, preferred_element_type=jnp.float32
    ).astype(jnp.bfloat16)
    return filled.reshape(panels, rows_here * block_edge, panel_width * block_edge)


def dense_right(values, columns, tile_width):
    panels, rows_here, tiles, slots, square = values.shape
    block_edge = math.isqrt(square)
    onehot = (
        columns.astype(jnp.float32)[..., None] == jnp.arange(tile_width, dtype=jnp.float32)
    ).astype(jnp.bfloat16)
    blocks = values.reshape(panels, rows_here, tiles, slots, block_edge, block_edge)
    filled = jnp.einsum(
        "qrtuc,qrtuab->qratcb", onehot, blocks, preferred_element_type=jnp.float32
    ).astype(jnp.bfloat16)
    return filled.reshape(panels, rows_here * block_edge, tiles * tile_width * block_edge)


def contract(left_values, left_codes, right_values, right_codes):
    left_filled = dense_left(left_values, left_codes, PANEL)
    right_filled = dense_right(
        lax.all_gather(right_values, "row", axis=1, tiled=True),
        lax.all_gather(right_codes, "row", axis=1, tiled=True),
        CTW,
    )
    return jnp.einsum("qmk,qkn->mn", left_filled, right_filled, preferred_element_type=jnp.float32)


def body(left_values, left_columns, right_values, right_columns):
    right_codes = right_columns.astype(jnp.bfloat16)
    partial_sums = contract(left_values, left_columns, right_values, right_codes)
    result = lax.psum_scatter(partial_sums, ("col", "depth"), scatter_dimension=1, tiled=True)
    return result.astype(jnp.bfloat16)


def solution(mesh):
    placed = (
        P("row", ("col", "depth"), None, None),
        P("row", ("col", "depth"), None),
        P(("col", "depth"), "row", None, None, None),
        P(("col", "depth"), "row", None, None),
    )
    return jax.shard_map(
        body, mesh=mesh, in_specs=placed, out_specs=P("row", ("col", "depth")), check_vma=False
    )
```

profile of v0, /device:TPU:0, one launch (start us, length us, event | category | flops | bytes accessed | tf_op | source)
XLA Modules:
  0.0 491.5 jit_solution(12231086556347016809)
XLA Ops:
  6.5 0.0 reduce-scatter.4.cloned.1.call-start
  6.5 21.0 %all_gather.7 = bf16[2,40,4,3,529]{4,2,3,1,0:T(4,128)(2,1)} all-gather(bf16[2,20,4,3,529]{4,2,3,1,0:T(4,128)(2,1)} %param.6), channel_id=1, replica_groups=mesh['row'=2,'col'=4,'depth'=4] {'row'}, dimensions={1}, use_global_device_ids=true | all-gather | bytes 1523520 | tf_op jit(solution)/shard_map/all_gather | solution.py:41
  27.5 4.9 %copy.32 = bf16[2,40,4,3,529]{1,2,4,3,0:T(4,128)(2,1)S(1)} copy(bf16[2,40,4,3,529]{4,2,3,1,0:T(4,128)(2,1)} %all_gather.7) | data formatting | bytes 2031360 | tf_op jit(solution)/shard_map/all_gather | solution.py:41
  32.4 11.9 %copy.33 = bf16[2,40,4,3,23,23]{5,3,4,2,1,0:T(4,128)(2,1)} copy(bf16[2,40,4,3,23,23]{1,2,5,4,3,0:T(4,128)(2,1)S(1)} %bitcast.33) | data formatting | bytes 2031360 | tf_op jit(solution)/shard_map/reshape | solution.py:31
  44.3 0.0 copy-done.1
  44.3 0.1 copy.29
  44.4 4.5 all_gather.6
  49.0 0.1 copy.30
  49.1 0.2 copy.31
  49.3 31.1 %convert_bitcast_fusion = bf16[2,40,23,4,32,23]{4,5,2,3,1,0:T(8,128)(2,1)} fusion(bf16[2,40,4,3,23,23]{5,3,4,2,1,0:T(4,128)(2,1)} %copy.33, f32[2,40,4,3]{3,2,1,0:T(4,128)S(1)} %copy.31), kind=kOutput, calls=%fused_computation | convolution fusion | flops 37949440 | bytes 11853440 | tf_op jit(solution)/shard_map/qrtuc,qrtuab->qratcb/dot_general | solution.py:32
  80.4 80.8 %copy.34 = bf16[2,40,23,4,32,23]{5,4,3,2,1,0:T(8,128)(2,1)} copy(bf16[2,40,23,4,32,23]{4,5,2,3,1,0:T(8,128)(2,1)} %convert_bitcast_fusion) | data formatting | bytes 21667840 | tf_op jit(solution)/shard_map/convert_element_type | solution.py:34
  161.2 70.7 %reshape.17 = bf16[2,920,2944]{2,1,0:T(8,128)(2,1)} reshape(bf16[2,40,23,4,32,23]{5,4,3,2,1,0:T(8,128)(2,1)} %copy.34) | data formatting | bytes 21667840 | tf_op jit(solution)/shard_map/reshape | solution.py:35
  231.9 0.0 copy-done
  231.9 1.7 copy.26
  233.6 3.6 copy.27
  237.2 0.0 copy-done.2
  237.2 0.1 copy.25
  237.3 10.2 %fusion = bf16[2,48,23,40,23]{3,4,2,1,0:T(8,128)(2,1)} fusion(bf16[48,2,4,23,23]{4,2,3,0,1:T(4,128)(2,1)S(1)} %copy.27, f32[48,2,4]{2,0,1:T(8,128)S(1)} %copy.25), kind=kOutput, calls=%fused_computation.3 | convolution fusion | flops 18297600 | bytes 4470528 | tf_op jit(solution)/shard_map/mqsp,mqsab->qmapb/dot_general | solution.py:19
  247.5 45.4 %copy.28 = bf16[2,48,23,40,23]{2,1,4,3,0:T(8,128)(2,1)} copy(bf16[2,48,23,40,23]{3,4,2,1,0:T(8,128)(2,1)} %fusion) | data formatting | bytes 8125440 | tf_op jit(solution)/shard_map/convert_element_type | solution.py:21
  292.9 27.5 %reshape.15 = bf16[2,1104,920]{1,2,0:T(8,128)(2,1)} reshape(bf16[2,48,23,40,23]{2,1,4,3,0:T(8,128)(2,1)} %copy.28) | data formatting | bytes 8125440 | tf_op jit(solution)/shard_map/reshape | solution.py:22
  320.3 21.8 %convolution_bitcast_fusion = f32[1104,2944]{0,1:T(8,128)} fusion(bf16[2,1104,920]{1,2,0:T(8,128)(2,1)} %reshape.15, bf16[2,920,2944]{2,1,0:T(8,128)(2,1)} %reshape.17), kind=kOutput, calls=%fused_computation.2 | convolution fusion | flops 11960647680 | bytes 27897344 | tf_op jit(solution)/shard_map/qmk,qkn->mn/dot_general | solution.py:45
  342.1 0.0 reduce-scatter.4.cloned.1.call-update
  342.1 140.6 %reduce-scatter.4.cloned.1.call-done = f32[1104,184]{0,1:T(8,128)} async-done(((f32[1104,2944]{0,1:T(8,128)}), f32[1104,184]{0,1:T(8,128)}) %reduce-scatter.4.cloned.1.call-update) | async-done | bytes 812560
  482.7 2.0 convert_element_type.33
  (5 shorter events, 0.0 us)
Async XLA Ops:
  6.5 476.1 %reduce-scatter.4.cloned.1.call-start = ((), (), s32[]{:S(2)}) async-start(), calls=%async_computation.1 | async-start | bytes 14413824
  27.5 16.8 %copy-start.1 = (s32[2,20,4,3]{1,2,3,0:T(4,128)S(1)}, s32[2,20,4,3]{1,2,3,0:T(4,128)}, u32[]{:S(2)}) copy-start(s32[2,20,4,3]{1,2,3,0:T(4,128)} %param.7) | copy-start | bytes 5764
  161.2 70.7 %copy-start = (bf16[48,2,4,529]{3,2,1,0:T(4,128)(2,1)S(1)}, bf16[48,2,4,529]{3,2,1,0:T(4,128)(2,1)}, u32[]{:S(2)}) copy-start(bf16[48,2,4,529]{3,2,1,0:T(4,128)(2,1)} %param.4) | copy-start | bytes 1218820
  161.2 75.9 %copy-start.2 = (s32[48,2,4]{0,2,1:T(4,128)S(1)}, s32[48,2,4]{0,2,1:T(4,128)}, u32[]{:S(2)}) copy-start(s32[48,2,4]{0,2,1:T(4,128)} %param.5) | copy-start | bytes 4612
Sparse Core Ops, SparseCore 0:
  342.2 140.3 reduce-scatter.3
where the time goes:
time: 497 us; the launch traced here: 491 us
  local copies, waits for them, and re-layouts  247 us (50%)
  waiting for transfers between devices  141 us (28%)
  matrix products  63.1 us (13%)
  blocking collectives  25.5 us (5%)
  between operations  13.4 us (3%)
    unnamed x2, waiting for transfers between devices  141 us
    convert_element_type x1, local copies, waits for them, and re-layouts, dense_right(): filled = jnp.einsum('qrtuc,qrtuab->qratcb', onehot, blocks, preferred_ele...  80.8 us
    reshape x1, local copies, waits for them, and re-layouts, dense_right(): filled.reshape(panels, rows_here * block_edge, tiles * tile_width * block...  70.7 us
    convert_element_type x1, local copies, waits for them, and re-layouts, dense_left(): filled = jnp.einsum('mqsp,mqsab->qmapb', onehot, blocks, preferred_elemen...  45.4 us
    dot_general x1, matrix products, dense_right(): jnp.einsum('qrtuc,qrtuab->qratcb', onehot, blocks, preferred_element_type...  31.1 us
    reshape x1, local copies, waits for them, and re-layouts, dense_left(): filled.reshape(panels, rows_here * block_edge, panel_width * block_edge)  27.5 us
    dot_general x1, matrix products, contract(): jnp.einsum('qmk,qkn->mn', left_filled, right_filled, preferred_element_ty...  21.8 us
    all_gather x1, blocking collectives, contract(): lax.all_gather(right_values, 'row', axis=1, tiled=True)  21 us
  transfers between devices with their start and end apart: 1, of which 1 were waited for; matrix products, arithmetic and copies ran while one was open for 0% of the time, Pallas kernels for 0%

commit v1 on v0

v1 whole, which is shorter than its diff:
```python
import functools
import math

import jax
import jax.numpy as jnp
from jax import lax
from jax.experimental import pallas as pl
from jax.experimental.pallas import tpu as pltpu
from jax.sharding import PartitionSpec as P

CTW = 32


def lay_left(values, columns):
    rows, panels, slots, square = values.shape
    edge = math.isqrt(square)
    blocks = values.reshape(rows, panels, slots, edge, edge).transpose(1, 2, 4, 0, 3)
    blocks = blocks.reshape(panels, slots, edge, rows * edge)
    codes = jnp.repeat(columns.transpose(1, 2, 0).astype(jnp.bfloat16), edge, axis=2)
    return jnp.concatenate([blocks, codes[:, :, None, :]], axis=2)


def lay_right(values, columns):
    panels, rows, tiles, slots, square = values.shape
    edge = math.isqrt(square)
    blocks = values.reshape(panels, rows, tiles, slots, edge, edge).transpose(2, 0, 3, 5, 1, 4)
    blocks = jnp.pad(blocks, ((0, 0),) * 5 + ((0, 1),))
    blocks = blocks.reshape(tiles, panels, slots, edge, rows * (edge + 1))
    codes = jnp.repeat(columns.transpose(2, 0, 3, 1).astype(jnp.bfloat16), edge + 1, axis=3)
    return jnp.concatenate([blocks, codes[:, :, :, None, :]], axis=3)


def expand(values_ref, lead, slots, pad, count, out_ref, base):
    width = out_ref.shape[-1]
    lower = lax.broadcasted_iota(jnp.int32, (2 * pad, width), 0) >= pad
    shift = jnp.where(lower, 1.0, 0.0)
    doubled, codes = [], []
    for s in range(slots):
        one = values_ref[lead + (s,)].astype(jnp.float32)
        code = jnp.broadcast_to(one[pad - 1 : pad, :], (2 * pad, width)) - shift
        doubled.append(jnp.concatenate([one, one], axis=0).astype(jnp.bfloat16))
        codes.append(code.astype(jnp.bfloat16))
    for pair in range(count // 2):
        want = jnp.bfloat16(base + 2 * pair)
        filled = jnp.zeros((2 * pad, width), jnp.bfloat16)
        for s in range(slots):
            filled = jnp.where(codes[s] == want, doubled[s], filled)
        out_ref[2 * pad * pair : 2 * pad * (pair + 1), :] = filled


def product_kernel(pad, left_ref, right_ref, out_ref, left_dense, right_dense):
    @pl.when(pl.program_id(0) == 0)
    def _():
        out_ref[...] = jnp.zeros_like(out_ref)

    parts, _, slots_r = right_ref.shape[:3]
    slots_l = left_ref.shape[1]
    here = left_dense.shape[1] // pad
    for r in range(parts):
        expand(left_ref, (0,), slots_l, pad, here, left_dense.at[r], r * here)
        expand(right_ref, (r, 0), slots_r, pad, CTW, right_dense.at[r], 0)
    total = out_ref[...]
    for r in range(parts):
        total += jnp.dot(right_dense[r], left_dense[r], preferred_element_type=jnp.float32)
    out_ref[...] = total


def product(left, right, pad):
    panels, slots_l, _, m = left.shape
    parts, _, slots_r, _, k = right.shape
    n = CTW * pad
    return pl.pallas_call(
        functools.partial(product_kernel, pad),
        grid=(panels,),
        in_specs=[
            pl.BlockSpec((1, slots_l, pad, m), lambda p: (p, 0, 0, 0)),
            pl.BlockSpec((parts, 1, slots_r, pad, k), lambda p: (0, p, 0, 0, 0)),
        ],
        out_specs=pl.BlockSpec((n, m), lambda p: (0, 0)),
        out_shape=jax.ShapeDtypeStruct((n, m), jnp.float32),
        scratch_shapes=[pltpu.VMEM((parts, k, m), jnp.bfloat16), pltpu.VMEM((parts, n, k), jnp.bfloat16)],
        compiler_params=pltpu.CompilerParams(vmem_limit_bytes=56 << 20),
    )(left, right)


def body(left_values, left_columns, right_values, right_columns):
    pad = math.isqrt(left_values.shape[-1]) + 1
    left = lax.all_gather(lay_left(left_values, left_columns), "col", axis=0, tiled=True)
    right = lax.all_to_all(lay_right(right_values, right_columns), "col", 0, 0, tiled=True)
    tiles, panels, slots, _, k = right.shape
    right = lax.all_gather(right.reshape(tiles * panels, slots, pad, k), "row", axis=0)
    if right_values.shape[1] % 2:
        parts = right.shape[0]
        right = right.transpose(1, 2, 3, 0, 4).reshape(1, tiles * panels, slots, pad, parts * k)
    partial_sums = product(left, right, pad)
    result = lax.psum_scatter(partial_sums, "depth", scatter_dimension=0, tiled=True)
    rows, m = result.shape
    result = result.reshape(rows // pad, pad, m)[:, : pad - 1].reshape(rows // pad * (pad - 1), m)
    return result.T.astype(jnp.bfloat16)


def solution(mesh):
    placed = (
        P("row", ("col", "depth"), None, None),
        P("row", ("col", "depth"), None),
        P(("col", "depth"), "row", None, None, None),
        P(("col", "depth"), "row", None, None),
    )
    return jax.shard_map(
        body, mesh=mesh, in_specs=placed, out_specs=P("row", ("col", "depth")), check_vma=False
    )
```

time: 497 us -> 183 us (0.37); the launches traced: 491 us -> 183 us
  local copies, waits for them, and re-layouts: 247 us -> 26.4 us
  matrix products: 63.1 us -> 0 us
  waiting for transfers between devices: 141 us -> 104 us
  Pallas kernels: 0 us -> 22.4 us
  blocking collectives: 25.5 us -> 13.7 us
    unnamed x2 -> x3, waiting for transfers between devices: 141 us -> 0.05 us
    convert_element_type x5 -> x2, local copies, waits for them, and re-layouts: 127 us -> 0.95 us  [the longest x1 0.94 us: body(): return result.T.astype(jnp.bfloat16)]
    reshape x4 -> x3, local copies, waits for them, and re-layouts: 114 us -> 11.8 us  [the longest x1 4.92 us: lay_right(): values.reshape(panels, rows, tiles, slots, edge, edge)]
    reduce_scatter x0 -> x1, waiting for transfers between devices: none -> 66.7 us  [body(): lax.psum_scatter(partial_sums, 'depth', scatter_dimension=0, tiled=True)]
    dot_general x3 -> x0, matrix products: 63.1 us -> none  [the longest x1 31.1 us: dense_right(): jnp.einsum('qrtuc,qrtuab->qratcb', onehot, blocks, preferred_element_type...]
    all_gather x0 -> x2, waiting for transfers between devices: none -> 37.8 us  [the longest x1 22.3 us: body(): lax.all_gather(lay_left(left_values, left_columns), 'col', axis=0, tiled=...]
    all_gather x2 -> x0, blocking collectives: 25.5 us -> none  [the longest x1 21 us: contract(): lax.all_gather(right_values, 'row', axis=1, tiled=True)]
    pallas_call x0 -> x1, Pallas kernels: none -> 22.4 us  [product(): pl.pallas_call(functools.partial(product_kernel, pad), grid=(panels,), in...]
  transfers between devices with their start and end apart: 1 -> 3, of which waited for: 1 -> 3; matrix products, arithmetic and copies ran while one was open for 0% -> 4% of each run, Pallas kernels for 0% -> 0%
where the time goes in v1:
time: 183 us
  waiting for transfers between devices  104 us (57%)
  local copies, waits for them, and re-layouts  26.4 us (14%)
  Pallas kernels  22.4 us (12%)
  blocking collectives  13.7 us (7%)
  between operations  13.2 us (7%)
  other arithmetic  2.22 us (1%)
    reduce_scatter x1, waiting for transfers between devices, body(): lax.psum_scatter(partial_sums, 'depth', scatter_dimension=0, tiled=True)  66.7 us
    pallas_call x1, Pallas kernels, product(): pl.pallas_call(functools.partial(product_kernel, pad), grid=(panels,), in...  22.4 us
    all_gather x1, waiting for transfers between devices, body(): lax.all_gather(lay_left(left_values, left_columns), 'col', axis=0, tiled=...  22.3 us
    all_gather x1, waiting for transfers between devices, body(): lax.all_gather(right.reshape(tiles * panels, slots, pad, k), 'row', axis=0)  15.5 us
    all_to_all x1, blocking collectives, body(): lax.all_to_all(lay_right(right_values, right_columns), 'col', 0, 0, tiled...  13.7 us
    unnamed x8, local copies, waits for them, and re-layouts  8.02 us
    reshape x1, local copies, waits for them, and re-layouts, lay_right(): values.reshape(panels, rows, tiles, slots, edge, edge)  4.92 us
    reshape x1, local copies, waits for them, and re-layouts, lay_right(): blocks = blocks.reshape(tiles, panels, slots, edge, rows * (edge + 1))  4.3 us
  transfers between devices with their start and end apart: 3, of which 3 were waited for; matrix products, arithmetic and copies ran while one was open for 4% of the time, Pallas kernels for 0%

profile of v1, /device:TPU:0, one launch (start us, length us, event | category | flops | bytes accessed | tf_op | source)
XLA Modules:
  0.0 182.5 jit_solution(5123523646040763906)
XLA Ops:
  6.5 4.9 %reshape.20 = bf16[2,20,4,3,23,23]{5,4,2,3,1,0:T(8,128)(2,1)} reshape(bf16[2,20,4,3,529]{4,2,3,1,0:T(4,128)(2,1)} %param.6) | data formatting | bytes 1015680 | tf_op jit(solution)/shard_map/reshape | solution.py:26
  11.5 6.3 %copy.20 = bf16[4,2,3,23,20,23]{5,4,3,2,1,0:T(8,128)(2,1)S(1)} copy(bf16[4,2,3,23,20,23]{3,5,0,2,4,1:T(8,128)(2,1)} %bitcast.20) | data formatting | bytes 1015680
  17.8 2.4 %pad.4.clone = bf16[4,2,3,23,20,24]{5,4,3,2,1,0:T(8,128)(2,1)} pad(bf16[4,2,3,23,20,23]{5,4,3,2,1,0:T(8,128)(2,1)S(1)} %copy.20, bf16[]{:T(256)} %constant.2.clone.1), padding=0_0x0_0x0_0x0_0x0_0x0_1 | pad | bytes 1037762 | tf_op jit(solution)/shard_map/jit(_pad)/pad | solution.py:27
  20.2 4.3 %reshape.21 = bf16[4,2,3,23,480]{4,3,2,1,0:T(8,128)(2,1)S(1)} reshape(bf16[4,2,3,23,20,24]{5,4,3,2,1,0:T(8,128)(2,1)} %pad.4.clone) | data formatting | bytes 1059840 | tf_op jit(solution)/shard_map/reshape | solution.py:28
  24.6 0.1 broadcast_in_dim.7
  24.7 0.2 broadcast_in_dim_reshape.7
  24.9 0.2 pad_maximum_fusion
  25.1 13.7 %all_to_all.5 = bf16[4,2,3,24,480]{4,3,2,1,0:T(8,128)(2,1)} all-to-all(bf16[4,2,3,24,480]{4,3,2,1,0:T(8,128)(2,1)S(1)} %pad_maximum_fusion), channel_id=1, replica_groups=mesh['row'=2,'col'=4,'depth'=4] {'col'}, dimensions={0} | all-to-all | bytes 1105920 | tf_op jit(solution)/shard_map/all_to_all | solution.py:89
  38.8 0.0 all-gather.5.cloned.1.call-update
  38.8 0.0 all-gather.3.cloned.1.call-start
  38.9 1.7 copy.14
  40.6 2.6 %copy.15 = bf16[2,4,23,48,23]{4,3,2,1,0:T(8,128)(2,1)S(1)} copy(bf16[2,4,23,48,23]{3,1,2,4,0:T(4,128)(2,1)S(1)} %bitcast.21) | data formatting | bytes 812544 | tf_op jit(solution)/shard_map/transpose | solution.py:17
  43.2 2.5 %reshape.19 = bf16[2,4,23,1104]{3,2,1,0:T(8,128)(2,1)S(1)} reshape(bf16[2,4,23,48,23]{4,3,2,1,0:T(8,128)(2,1)S(1)} %copy.15) | data formatting | bytes 812544 | tf_op jit(solution)/shard_map/reshape | solution.py:18
  45.7 0.1 broadcast_in_dim.6
  45.9 0.2 broadcast_in_dim_reshape.8
  46.0 0.8 pad_maximum_fusion.1
  46.9 0.0 all-gather.3.cloned.1.call-update
  46.9 0.0 reduce-scatter.2.cloned.1.call-start
  46.9 15.5 %all-gather.5.cloned.1.call-done.right_ref = bf16[2,8,3,24,480]{4,3,2,1,0:T(8,128)(2,1)} async-done(((bf16[1,8,3,24,480]{4,3,2,1,0:T(8,128)(2,1)}), bf16[2,8,3,24,480]{4,3,2,1,0:T(8,128)(2,1)}) %all-gather.5.cloned.1.call-update) | async-done | bytes 1105936 | tf_op jit(solution)/shard_map/all_gather | solution.py:91
  62.4 22.3 %all-gather.3.cloned.1.call-done.left_ref = bf16[8,4,24,1104]{3,2,1,0:T(8,128)(2,1)} async-done(((bf16[2,4,24,1104]{3,2,1,0:T(8,128)(2,1)}), bf16[8,4,24,1104]{3,2,1,0:T(8,128)(2,1)}) %all-gather.3.cloned.1.call-update) | async-done | bytes 1695760 | tf_op jit(solution)/shard_map/all_gather | solution.py:88
  84.7 22.4 %shard_map.46 = f32[768,1104]{1,0:T(8,128)} custom-call(bf16[8,4,24,1104]{3,2,1,0:T(8,128)(2,1)} %all-gather.3.cloned.1.call-done.left_ref, bf16[2,8,3,24,480]{4,3,2,1,0:T(8,128)(2,1)} %all-gather.5.cloned.1.call-done.right_ref), custom_call_target="tpu_custom_call" | custom-call | tf_op jit(solution)/shard_map/pallas_call | solution.py:72
  107.2 66.7 %reduce-scatter.2.cloned.1.call-done = f32[192,1104]{1,0:T(8,128)} async-done(((f32[768,1104]{1,0:T(8,128)}), f32[192,1104]{1,0:T(8,128)}) %reduce-scatter.2.cloned.1.call-update) | async-done | bytes 847888 | tf_op jit(solution)/shard_map/reduce_scatter | solution.py:96
  173.8 1.2 convert.4
  175.1 0.9 convert_element_type.25
  (12 shorter events, 0.1 us)
Async XLA Ops:
  6.5 55.9 %all-gather.5.cloned.1.call-start = ((), (), s32[]{:S(2)}) async-start(), calls=%async_computation.3 | async-start | bytes 1769472 | tf_op jit(solution)/shard_map/all_gather | solution.py:91
  20.2 4.3 %copy-start.1 = (s32[2,20,4,3]{1,2,3,0:T(4,128)S(1)}, s32[2,20,4,3]{1,2,3,0:T(4,128)}, u32[]{:S(2)}) copy-start(s32[2,20,4,3]{1,2,3,0:T(4,128)} %param.7) | copy-start | bytes 5764
  24.5 14.3 %copy-start = (bf16[48,2,4,529]{3,2,1,0:T(4,128)(2,1)S(1)}, bf16[48,2,4,529]{3,2,1,0:T(4,128)(2,1)}, u32[]{:S(2)}) copy-start(bf16[48,2,4,529]{3,2,1,0:T(4,128)(2,1)} %param.4) | copy-start | bytes 1218820
  38.8 45.9 %all-gather.3.cloned.1.call-start = ((), (), s32[]{:S(2)}) async-start(), calls=%async_computation.2 | async-start | bytes 2211840 | tf_op jit(solution)/shard_map/all_gather | solution.py:88
  43.2 2.6 %copy-start.2 = (s32[48,2,4]{0,2,1:T(4,128)S(1)}, s32[48,2,4]{0,2,1:T(4,128)}, u32[]{:S(2)}) copy-start(s32[48,2,4]{0,2,1:T(4,128)} %param.5) | copy-start | bytes 4612
  46.9 126.9 %reduce-scatter.2.cloned.1.call-start = ((), (), s32[]{:S(2)}) async-start(), calls=%async_computation.4 | async-start | bytes 4423680 | tf_op jit(solution)/shard_map/reduce_scatter | solution.py:96
Sparse Core Ops, SparseCore 0:
  38.9 23.4 all-gather.4
  64.0 20.7 all-gather.2
  107.3 66.4 reduce-scatter.1

commit v2 on v1

--- a/solution.py
+++ b/solution.py
@@ -83,17 +83,81 @@
     )(left, right)
 
 
-def body(left_values, left_columns, right_values, right_columns):
+def ring_kernel(streams, own_ref, out_ref, landed, send_sem, recv_sem):
+    n = own_ref.shape[0]
+    me = lax.axis_index("depth")
+    after, before = lax.rem(me + 1, n), lax.rem(me + n - 1, n)
+    barrier = pltpu.get_barrier_semaphore()
+    for other in (before, after):
+        pl.semaphore_signal(barrier, inc=1, device_id={"depth": other}, device_id_type=pl.DeviceIdType.MESH)
+    pl.semaphore_wait(barrier, 2)
+
+    rows = own_ref.shape[1] // streams
+    spans = [pl.ds(rows * i, rows) for i in range(streams)]
+
+    def hop(step, i, source):
+        return pltpu.make_async_remote_copy(
+            src_ref=source,
+            dst_ref=landed.at[step, spans[i]],
+            send_sem=send_sem.at[step, i],
+            recv_sem=recv_sem.at[step, i],
+            device_id={"depth": before if i % 2 else after},
+            device_id_type=pl.DeviceIdType.MESH,
+        )
+
+    def chunk(step, i):
+        return lax.rem(me + 1 + step, n) if i % 2 else lax.rem(me + 2 * n - 1 - step, n)
+
+    hops = {}
+    for i in range(streams):
+        hops[0, i] = hop(0, i, own_ref.at[chunk(0, i), spans[i]])
+        hops[0, i].start()
+    for step in range(n - 1):
+        for i in range(streams):
+            hops[step, i].wait_recv()
+            total = landed[step, spans[i], :] + own_ref[chunk(step + 1, i), spans[i], :]
+            if step == n - 2:
+                out_ref[spans[i], :] = total
+            else:
+                landed[step, spans[i], :] = total
+                hops[step + 1, i] = hop(step + 1, i, landed.at[step, spans[i]])
+                hops[step + 1, i].start()
+    for each in hops.values():
+        each.wait_send()
+
+
+def ring_sum(partial_sums, n):
+    rows, m = partial_sums.shape[0] // n, partial_sums.shape[1]
+    streams = 4
+    whole = pl.BlockSpec(memory_space=pltpu.VMEM)
+    return pl.pallas_call(
+        functools.partial(ring_kernel, streams),
+        in_specs=[whole],
+        out_specs=whole,
+        out_shape=jax.ShapeDtypeStruct((rows, m), jnp.float32),
+        scratch_shapes=[
+            pltpu.VMEM((n - 1, rows, m), jnp.float32),
+            pltpu.SemaphoreType.DMA((n - 1, streams)),
+            pltpu.SemaphoreType.DMA((n - 1, streams)),
+        ],
+        compiler_params=pltpu.CompilerParams(collective_id=0, has_side_effects=True, vmem_limit_bytes=32 << 20),
+    )(partial_sums.reshape(n, rows, m))
+
+
+def body(depth, left_values, left_columns, right_values, right_columns):
     pad = math.isqrt(left_values.shape[-1]) + 1
-    left = lax.all_gather(lay_left(left_values, left_columns), "col", axis=0, tiled=True)
-    right = lax.all_to_all(lay_right(right_values, right_columns), "col", 0, 0, tiled=True)
+    left = lay_left(left_values, left_columns)
+    left, right_values = lax.optimization_barrier((left, right_values))
+    left = lax.all_gather(left, "col", axis=0, tiled=True)
+    left, right = lax.optimization_barrier((left, lay_right(right_values, right_columns)))
+    right = lax.all_to_all(right, "col", 0, 0, tiled=True)
     tiles, panels, slots, _, k = right.shape
     right = lax.all_gather(right.reshape(tiles * panels, slots, pad, k), "row", axis=0)
     if right_values.shape[1] % 2:
         parts = right.shape[0]
         right = right.transpose(1, 2, 3, 0, 4).reshape(1, tiles * panels, slots, pad, parts * k)
     partial_sums = product(left, right, pad)
-    result = lax.psum_scatter(partial_sums, "depth", scatter_dimension=0, tiled=True)
+    result = ring_sum(partial_sums, depth)
     rows, m = result.shape
     result = result.reshape(rows // pad, pad, m)[:, : pad - 1].reshape(rows // pad * (pad - 1), m)
     return result.T.astype(jnp.bfloat16)
@@ -107,5 +171,5 @@
         P(("col", "depth"), "row", None, None),
     )
     return jax.shard_map(
-        body, mesh=mesh, in_specs=placed, out_specs=P("row", ("col", "depth")), check_vma=False
+        functools.partial(body, mesh.shape["depth"]), mesh=mesh, in_specs=placed, out_specs=P("row", ("col", "depth")), check_vma=False
     )

time: 183 us -> 168 us (0.918)
  waiting for transfers between devices: 104 us -> 29.1 us
  Pallas kernels: 22.4 us -> 82.9 us
  local copies, waits for them, and re-layouts: 26.4 us -> 28.4 us
    reduce_scatter x1 -> x0, waiting for transfers between devices: 66.7 us -> none  [body(): lax.psum_scatter(partial_sums, 'depth', scatter_dimension=0, tiled=True)]
    pallas_call x0 -> x1, Pallas kernels: none -> 60.4 us  [ring_sum(): pl.pallas_call(functools.partial(ring_kernel, streams), in_specs=[whole],...]
    all_gather x1, waiting for transfers between devices: 22.3 us -> 6.14 us  [body(): left = lax.all_gather(left, 'col', axis=0, tiled=True)]
    all_gather x1, waiting for transfers between devices: 15.5 us -> 22.9 us  [body(): lax.all_gather(right.reshape(tiles * panels, slots, pad, k), 'row', axis=0)]
    unnamed x8 -> x10, local copies, waits for them, and re-layouts: 8.02 us -> 11.3 us
  transfers between devices with their start and end apart: 3 -> 2, of which waited for: 3 -> 2; matrix products, arithmetic and copies ran while one was open for 4% -> 10% of each run, Pallas kernels for 0% -> 0%
where the time goes in v2:
time: 168 us
  Pallas kernels  82.9 us (49%)
  waiting for transfers between devices  29.1 us (17%)
  local copies, waits for them, and re-layouts  28.4 us (17%)
  between operations  13.6 us (8%)
  blocking collectives  12.6 us (8%)
    pallas_call x1, Pallas kernels, ring_sum(): pl.pallas_call(functools.partial(ring_kernel, streams), in_specs=[whole],...  60.4 us
    all_gather x1, waiting for transfers between devices, body(): lax.all_gather(right.reshape(tiles * panels, slots, pad, k), 'row', axis=0)  22.9 us
    pallas_call x1, Pallas kernels, product(): pl.pallas_call(functools.partial(product_kernel, pad), grid=(panels,), in...  22.4 us
    all_to_all x1, blocking collectives, body(): right = lax.all_to_all(right, 'col', 0, 0, tiled=True)  12.6 us
    unnamed x10, local copies, waits for them, and re-layouts  11.3 us
    all_gather x1, waiting for transfers between devices, body(): left = lax.all_gather(left, 'col', axis=0, tiled=True)  6.14 us
    reshape x1, local copies, waits for them, and re-layouts, lay_right(): blocks = blocks.reshape(tiles, panels, slots, edge, rows * (edge + 1))  4.3 us
    reshape x1, local copies, waits for them, and re-layouts, lay_right(): values.reshape(panels, rows, tiles, slots, edge, edge)  3.76 us
  transfers between devices with their start and end apart: 2, of which 2 were waited for; matrix products, arithmetic and copies ran while one was open for 10% of the time, Pallas kernels for 0%

profile of v2, /device:TPU:0, one launch (start us, length us, event | category | flops | bytes accessed | tf_op | source)
XLA Modules:
  0.0 167.6 jit_solution(16437998554963636230)
XLA Ops:
  6.5 3.0 %copy.14 = bf16[48,2,4,529]{0,2,3,1:T(4,128)(2,1)S(1)} copy(bf16[48,2,4,529]{3,2,1,0:T(4,128)(2,1)} %param.4) | data formatting | bytes 812544 | tf_op args[0]
  9.5 2.6 %copy.15 = bf16[2,4,23,48,23]{4,3,2,1,0:T(8,128)(2,1)S(1)} copy(bf16[2,4,23,48,23]{3,1,2,4,0:T(4,128)(2,1)S(1)} %bitcast.23) | data formatting | bytes 812544 | tf_op jit(solution)/shard_map/transpose | solution.py:17
  12.1 2.4 %reshape.22 = bf16[2,4,23,1104]{3,2,1,0:T(8,128)(2,1)S(1)} reshape(bf16[2,4,23,48,23]{4,3,2,1,0:T(8,128)(2,1)S(1)} %copy.15) | data formatting | bytes 812544 | tf_op jit(solution)/shard_map/reshape | solution.py:18
  14.6 0.1 broadcast_in_dim.6
  14.7 0.2 broadcast_in_dim_reshape.8
  14.9 0.9 pad_maximum_fusion.1
  15.8 0.0 all-gather.3.cloned.1.call-update
  15.8 0.0 all-gather.5.cloned.1.call-start
  15.8 3.8 %reshape.23 = bf16[2,20,4,3,23,23]{5,4,2,3,1,0:T(8,128)(2,1)} reshape(bf16[2,20,4,3,529]{4,2,3,1,0:T(4,128)(2,1)S(1)} %copy-done.1) | data formatting | bytes 1015680 | tf_op jit(solution)/shard_map/reshape | solution.py:26
  19.6 6.3 %copy.20 = bf16[4,2,3,23,20,23]{5,4,3,2,1,0:T(8,128)(2,1)S(1)} copy(bf16[4,2,3,23,20,23]{3,5,0,2,4,1:T(8,128)(2,1)} %bitcast.22) | data formatting | bytes 1015680
  25.9 2.4 %pad.4.clone = bf16[4,2,3,23,20,24]{5,4,3,2,1,0:T(8,128)(2,1)} pad(bf16[4,2,3,23,20,23]{5,4,3,2,1,0:T(8,128)(2,1)S(1)} %copy.20, bf16[]{:T(256)} %constant.2.clone.1), padding=0_0x0_0x0_0x0_0x0_0x0_1 | pad | bytes 1037762 | tf_op jit(solution)/shard_map/jit(_pad)/pad | solution.py:27
  28.4 4.3 %reshape.24 = bf16[4,2,3,23,480]{4,3,2,1,0:T(8,128)(2,1)S(1)} reshape(bf16[4,2,3,23,20,24]{5,4,3,2,1,0:T(8,128)(2,1)} %pad.4.clone) | data formatting | bytes 1059840 | tf_op jit(solution)/shard_map/reshape | solution.py:28
  32.7 0.1 broadcast_in_dim.7
  32.9 0.2 broadcast_in_dim_reshape.7
  33.1 0.2 pad_maximum_fusion
  33.3 6.1 %all-gather.3.cloned.1.call-done.left_ref = bf16[8,4,24,1104]{3,2,1,0:T(8,128)(2,1)} async-done(((bf16[2,4,24,1104]{3,2,1,0:T(8,128)(2,1)}), bf16[8,4,24,1104]{3,2,1,0:T(8,128)(2,1)}) %all-gather.3.cloned.1.call-update) | async-done | bytes 1695760 | tf_op jit(solution)/shard_map/all_gather | solution.py:151
  39.4 12.6 %all_to_all.5 = bf16[4,2,3,24,480]{4,3,2,1,0:T(8,128)(2,1)} all-to-all(bf16[4,2,3,24,480]{4,3,2,1,0:T(8,128)(2,1)S(1)} %pad_maximum_fusion), channel_id=1, replica_groups=mesh['row'=2,'col'=4,'depth'=4] {'col'}, dimensions={0} | all-to-all | bytes 1105920 | tf_op jit(solution)/shard_map/all_to_all | solution.py:153
  52.0 0.0 all-gather.5.cloned.1.call-update
  52.0 22.9 %all-gather.5.cloned.1.call-done.right_ref = bf16[2,8,3,24,480]{4,3,2,1,0:T(8,128)(2,1)} async-done(((bf16[1,8,3,24,480]{4,3,2,1,0:T(8,128)(2,1)}), bf16[2,8,3,24,480]{4,3,2,1,0:T(8,128)(2,1)}) %all-gather.5.cloned.1.call-update) | async-done | bytes 1105936 | tf_op jit(solution)/shard_map/all_gather | solution.py:155
  74.9 22.4 %shard_map.46 = f32[768,1104]{1,0:T(8,128)} custom-call(bf16[8,4,24,1104]{3,2,1,0:T(8,128)(2,1)} %all-gather.3.cloned.1.call-done.left_ref, bf16[2,8,3,24,480]{4,3,2,1,0:T(8,128)(2,1)} %all-gather.5.cloned.1.call-done.right_ref), custom_call_target="tpu_custom_call" | custom-call | tf_op jit(solution)/shard_map/pallas_call | solution.py:72
  97.3 2.0 %copy-done = f32[768,1104]{1,0:T(8,128)S(1)} copy-done((f32[768,1104]{1,0:T(8,128)S(1)}, f32[768,1104]{1,0:T(8,128)}, u32[]{:S(2)}) %copy-start) | copy-done | bytes 3391512
  99.3 60.4 %shard_map.47 = f32[192,1104]{1,0:T(8,128)S(1)} custom-call(f32[4,192,1104]{2,1,0:T(8,128)S(1)} %bitcast.21), custom_call_target="tpu_custom_call" | custom-call | tf_op jit(solution)/shard_map/pallas_call | solution.py:133
  159.8 0.1 convert.4
  159.8 0.9 convert_element_type.25
  (12 shorter events, 0.1 us)
Async XLA Ops:
  6.5 32.9 %all-gather.3.cloned.1.call-start = ((), (), s32[]{:S(2)}) async-start(), calls=%async_computation.1 | async-start | bytes 2211840 | tf_op jit(solution)/shard_map/all_gather | solution.py:151
  12.1 2.4 %copy-start.3 = (s32[48,2,4]{0,2,1:T(4,128)S(1)}, s32[48,2,4]{0,2,1:T(4,128)}, u32[]{:S(2)}) copy-start(s32[48,2,4]{0,2,1:T(4,128)} %param.5) | copy-start | bytes 4612
  12.1 3.7 %copy-start.1 = (bf16[2,20,4,3,529]{4,2,3,1,0:T(4,128)(2,1)S(1)}, bf16[2,20,4,3,529]{4,2,3,1,0:T(4,128)(2,1)}, u32[]{:S(2)}) copy-start(bf16[2,20,4,3,529]{4,2,3,1,0:T(4,128)(2,1)} %param.6) | copy-start | bytes 1523524
  15.8 59.1 %all-gather.5.cloned.1.call-start = ((), (), s32[]{:S(2)}) async-start(), calls=%async_computation.2 | async-start | bytes 1769472 | tf_op jit(solution)/shard_map/all_gather | solution.py:155
  28.4 4.3 %copy-start.2 = (s32[2,20,4,3]{1,2,3,0:T(4,128)S(1)}, s32[2,20,4,3]{1,2,3,0:T(4,128)}, u32[]{:S(2)}) copy-start(s32[2,20,4,3]{1,2,3,0:T(4,128)} %param.7) | copy-start | bytes 5764
  97.3 2.0 %copy-start = (f32[768,1104]{1,0:T(8,128)S(1)}, f32[768,1104]{1,0:T(8,128)}, u32[]{:S(2)}) copy-start(f32[768,1104]{1,0:T(8,128)} %shard_map.46) | copy-start | bytes 10174468
Sparse Core Ops, SparseCore 0:
  15.9 23.4 all-gather.2
  52.1 22.7 all-gather.4

commit v3 on v2

--- a/solution.py
+++ b/solution.py
@@ -83,6 +83,86 @@
     )(left, right)
 
 
+def gather_kernel(columns, rows, left_ref, right_ref, left_out, right_out, left_send, left_recv, tile_send, tile_recv, row_send, row_recv):
+    me_col, me_row = lax.axis_index("col"), lax.axis_index("row")
+    mesh_id = pl.DeviceIdType.MESH
+    barrier = pltpu.get_barrier_semaphore()
+    for d in range(1, columns):
+        pl.semaphore_signal(barrier, inc=1, device_id={"col": lax.rem(me_col + d, columns)}, device_id_type=mesh_id)
+    for d in range(1, rows):
+        pl.semaphore_signal(barrier, inc=1, device_id={"row": lax.rem(me_row + d, rows)}, device_id_type=mesh_id)
+    pl.semaphore_wait(barrier, columns + rows - 2)
+
+    tile_hops, left_hops, row_hops = [], [], []
+    for d in range(1, columns):
+        other = lax.rem(me_col + d, columns)
+        tile_hops.append(
+            pltpu.make_async_remote_copy(
+                src_ref=right_ref.at[other],
+                dst_ref=right_out.at[me_row, me_col],
+                send_sem=tile_send.at[d],
+                recv_sem=tile_recv.at[d],
+                device_id={"col": other},
+                device_id_type=mesh_id,
+            )
+        )
+        left_hops.append(
+            pltpu.make_async_remote_copy(
+                src_ref=left_ref,
+                dst_ref=left_out.at[me_col],
+                send_sem=left_send.at[d],
+                recv_sem=left_recv.at[d],
+                device_id={"col": other},
+                device_id_type=mesh_id,
+            )
+        )
+
+    def to_rows(d, source):
+        slot = lax.rem(me_col + columns - d, columns)
+        for e in range(1, rows):
+            hop = pltpu.make_async_remote_copy(
+                src_ref=source,
+                dst_ref=right_out.at[me_row, slot],
+                send_sem=row_send.at[e, d],
+                recv_sem=row_recv.at[e, d],
+                device_id={"row": lax.rem(me_row + e, rows)},
+                device_id_type=mesh_id,
+            )
+            hop.start()
+            row_hops.append(hop)
+
+    for hop in tile_hops:
+        hop.start()
+    to_rows(0, right_ref.at[me_col])
+    for hop in left_hops:
+        hop.start()
+    left_out[me_col] = left_ref[...]
+    right_out[me_row, me_col] = right_ref[me_col]
+    for d, hop in enumerate(tile_hops, 1):
+        hop.wait_recv()
+        to_rows(d, right_out.at[me_row, lax.rem(me_col + columns - d, columns)])
+    for hop in left_hops + row_hops:
+        hop.wait_recv()
+    for hop in tile_hops + left_hops + row_hops:
+        hop.wait_send()
+
+
+def gather(left, right, columns, rows):
+    whole = pl.BlockSpec(memory_space=pltpu.VMEM)
+    dma = pltpu.SemaphoreType.DMA
+    return pl.pallas_call(
+        functools.partial(gather_kernel, columns, rows),
+        in_specs=[whole, whole],
+        out_specs=[whole, whole],
+        out_shape=[
+            jax.ShapeDtypeStruct((columns,) + left.shape, left.dtype),
+            jax.ShapeDtypeStruct((rows,) + right.shape, right.dtype),
+        ],
+        scratch_shapes=[dma((columns,))] * 4 + [dma((rows, columns))] * 2,
+        compiler_params=pltpu.CompilerParams(collective_id=1, has_side_effects=True, vmem_limit_bytes=32 << 20),
+    )(left, right)
+
+
 def ring_kernel(streams, own_ref, out_ref, landed, send_sem, recv_sem):
     n = own_ref.shape[0]
     me = lax.axis_index("depth")
@@ -144,22 +224,20 @@
     )(partial_sums.reshape(n, rows, m))
 
 
-def body(depth, left_values, left_columns, right_values, right_columns):
+def body(columns, rows, depth, left_values, left_columns, right_values, right_columns):
     pad = math.isqrt(left_values.shape[-1]) + 1
-    left = lay_left(left_values, left_columns)
-    left, right_values = lax.optimization_barrier((left, right_values))
-    left = lax.all_gather(left, "col", axis=0, tiled=True)
-    left, right = lax.optimization_barrier((left, lay_right(right_values, right_columns)))
-    right = lax.all_to_all(right, "col", 0, 0, tiled=True)
-    tiles, panels, slots, _, k = right.shape
-    right = lax.all_gather(right.reshape(tiles * panels, slots, pad, k), "row", axis=0)
+    left, right = gather(
+        lay_left(left_values, left_columns), lay_right(right_values, right_columns), columns, rows
+    )
+    left = left.reshape((-1,) + left.shape[2:])
+    right = right.reshape((rows, -1) + right.shape[3:])
     if right_values.shape[1] % 2:
-        parts = right.shape[0]
-        right = right.transpose(1, 2, 3, 0, 4).reshape(1, tiles * panels, slots, pad, parts * k)
+        right = right.transpose(1, 2, 3, 0, 4)
+        right = right.reshape((1,) + right.shape[:3] + (-1,))
     partial_sums = product(left, right, pad)
     result = ring_sum(partial_sums, depth)
-    rows, m = result.shape
-    result = result.reshape(rows // pad, pad, m)[:, : pad - 1].reshape(rows // pad * (pad - 1), m)
+    kept, m = result.shape
+    result = result.reshape(kept // pad, pad, m)[:, : pad - 1].reshape(kept // pad * (pad - 1), m)
     return result.T.astype(jnp.bfloat16)
 
 
@@ -171,5 +249,5 @@
         P(("col", "depth"), "row", None, None),
     )
     return jax.shard_map(
-        functools.partial(body, mesh.shape["depth"]), mesh=mesh, in_specs=placed, out_specs=P("row", ("col", "depth")), check_vma=False
+        functools.partial(body, mesh.shape["col"], mesh.shape["row"], mesh.shape["depth"]), mesh=mesh, in_specs=placed, out_specs=P("row", ("col", "depth")), check_vma=False
     )

time: 168 us -> 146 us (0.87)
  Pallas kernels: 82.9 us -> 113 us
  waiting for transfers between devices: 29.1 us -> 0 us
  between operations: 13.6 us -> 0.17 us
  blocking collectives: 12.6 us -> 0 us
  local copies, waits for them, and re-layouts: 28.4 us -> 32.2 us
    pallas_call x0 -> x1, Pallas kernels: none -> 29.1 us  [gather(): pl.pallas_call(functools.partial(gather_kernel, columns, rows), in_specs=...]
    all_gather x2 -> x0, waiting for transfers between devices: 29 us -> none  [the longest x1 22.9 us: body(): lax.all_gather(right.reshape(tiles * panels, slots, pad, k), 'row', axis=0)]
    all_to_all x1 -> x0, blocking collectives: 12.6 us -> none  [body(): right = lax.all_to_all(right, 'col', 0, 0, tiled=True)]
    unnamed x10 -> x14, local copies, waits for them, and re-layouts: 11.3 us -> 13.2 us
  transfers between devices with their start and end apart: 2 -> 0, of which waited for: 2 -> 0; matrix products, arithmetic and copies ran while one was open for 10% -> 0% of each run, Pallas kernels for 0% -> 0%
where the time goes in v3:
time: 146 us
  Pallas kernels  113 us (77%)
  local copies, waits for them, and re-layouts  32.2 us (22%)
    pallas_call x1, Pallas kernels, ring_sum(): pl.pallas_call(functools.partial(ring_kernel, streams), in_specs=[whole],...  61.7 us
    pallas_call x1, Pallas kernels, gather(): pl.pallas_call(functools.partial(gather_kernel, columns, rows), in_specs=...  29.1 us
    pallas_call x1, Pallas kernels, product(): pl.pallas_call(functools.partial(product_kernel, pad), grid=(panels,), in...  22.4 us
    unnamed x14, local copies, waits for them, and re-layouts  13.2 us
    reshape x1, local copies, waits for them, and re-layouts, lay_right(): values.reshape(panels, rows, tiles, slots, edge, edge)  4.91 us
    reshape x1, local copies, waits for them, and re-layouts, lay_right(): blocks = blocks.reshape(tiles, panels, slots, edge, rows * (edge + 1))  4.3 us
    transpose x1, local copies, waits for them, and re-layouts, lay_left(): values.reshape(rows, panels, slots, edge, edge).transpose(1, 2, 4, 0, 3)  3.37 us

profile of v3, /device:TPU:0, one launch (start us, length us, event | category | flops | bytes accessed | tf_op | source)
XLA Modules:
  0.0 145.9 jit_solution(14355553327916610493)
XLA Ops:
  0.0 4.9 %reshape.29 = bf16[2,20,4,3,23,23]{5,4,2,3,1,0:T(8,128)(2,1)} reshape(bf16[2,20,4,3,529]{4,2,3,1,0:T(4,128)(2,1)} %param.6) | data formatting | bytes 1015680 | tf_op jit(solution)/shard_map/reshape | solution.py:26
  4.9 6.3 %copy.14 = bf16[4,2,3,23,20,23]{5,4,3,2,1,0:T(8,128)(2,1)S(1)} copy(bf16[4,2,3,23,20,23]{3,5,0,2,4,1:T(8,128)(2,1)} %bitcast.25) | data formatting | bytes 1015680
  11.2 2.5 %pad.4.clone = bf16[4,2,3,23,20,24]{5,4,3,2,1,0:T(8,128)(2,1)} pad(bf16[4,2,3,23,20,23]{5,4,3,2,1,0:T(8,128)(2,1)S(1)} %copy.14, bf16[]{:T(256)} %constant.2.clone.1), padding=0_0x0_0x0_0x0_0x0_0x0_1 | pad | bytes 1037762 | tf_op jit(solution)/shard_map/jit(_pad)/pad | solution.py:27
  13.7 4.3 %reshape.30 = bf16[4,2,3,23,480]{4,3,2,1,0:T(8,128)(2,1)S(1)} reshape(bf16[4,2,3,23,20,24]{5,4,3,2,1,0:T(8,128)(2,1)} %pad.4.clone) | data formatting | bytes 1059840 | tf_op jit(solution)/shard_map/reshape | solution.py:28
  18.0 0.0 copy-start.3
  18.0 0.1 broadcast_in_dim.7
  18.2 0.2 broadcast_in_dim_reshape.7
  18.4 0.2 pad_maximum_fusion.right_ref
  18.6 0.5 copy-done.3
  19.0 2.1 %copy.8 = bf16[48,2,4,529]{0,2,3,1:T(4,128)(2,1)} copy(bf16[48,2,4,529]{3,2,1,0:T(4,128)(2,1)S(1)} %copy-done.3) | data formatting | bytes 812544 | tf_op args[0]
  21.2 3.4 %copy.9 = bf16[2,4,23,48,23]{4,3,2,1,0:T(8,128)(2,1)S(1)} copy(bf16[2,4,23,48,23]{3,1,2,4,0:T(4,128)(2,1)} %bitcast.26) | data formatting | bytes 812544 | tf_op jit(solution)/shard_map/transpose | solution.py:17
  24.5 0.0 copy-start.5
  24.6 2.4 %reshape.28 = bf16[2,4,23,1104]{3,2,1,0:T(8,128)(2,1)S(1)} reshape(bf16[2,4,23,48,23]{4,3,2,1,0:T(8,128)(2,1)S(1)} %copy.9) | data formatting | bytes 812544 | tf_op jit(solution)/shard_map/reshape | solution.py:18
  27.0 0.1 broadcast_in_dim.6
  27.1 0.2 broadcast_in_dim_reshape.8
  27.3 0.1 pad_maximum_fusion.1.left_ref
  27.4 29.1 %shard_map.46 = (bf16[4,2,4,24,1104]{4,3,2,1,0:T(8,128)(2,1)S(1)}, bf16[2,4,2,3,24,480]{5,4,3,2,1,0:T(8,128)(2,1)S(1)}) custom-call(bf16[2,4,24,1104]{3,2,1,0:T(8,128)(2,1)S(1)} %pad_maximum_fusion.1.left_ref, bf16[4,2,3,24,480]{4,3,2,1,0:T(8,128)(2,1)S(1)} %pad_maximum_fusion.right_ref), custom_call_target="tpu_custom_call" | custom-call | tf_op jit(solution)/shard_map/pallas_call | solution.py:153
  56.5 1.2 copy-done.1
  57.7 1.1 copy-done.2
  58.8 22.4 %shard_map.47 = f32[768,1104]{1,0:T(8,128)} custom-call(bf16[8,4,24,1104]{3,2,1,0:T(8,128)(2,1)} %bitcast.23, bf16[2,8,3,24,480]{4,3,2,1,0:T(8,128)(2,1)} %bitcast.24), custom_call_target="tpu_custom_call" | custom-call | tf_op jit(solution)/shard_map/pallas_call | solution.py:72
  81.2 2.0 %copy-done = f32[768,1104]{1,0:T(8,128)S(1)} copy-done((f32[768,1104]{1,0:T(8,128)S(1)}, f32[768,1104]{1,0:T(8,128)}, u32[]{:S(2)}) %copy-start) | copy-done | bytes 3391512
  83.2 61.7 %shard_map.48 = f32[192,1104]{1,0:T(8,128)S(1)} custom-call(f32[4,192,1104]{2,1,0:T(8,128)S(1)} %bitcast.22), custom_call_target="tpu_custom_call" | custom-call | tf_op jit(solution)/shard_map/pallas_call | solution.py:213
  144.9 0.1 convert.4
  145.0 0.9 convert_element_type.25
  (10 shorter events, 0.1 us)
Async XLA Ops:
  13.7 4.3 %copy-start.4 = (s32[2,20,4,3]{1,2,3,0:T(4,128)S(1)}, s32[2,20,4,3]{1,2,3,0:T(4,128)}, u32[]{:S(2)}) copy-start(s32[2,20,4,3]{1,2,3,0:T(4,128)} %param.7) | copy-start | bytes 5764
  18.0 1.0 copy-start.3
  24.5 2.4 %copy-start.5 = (s32[48,2,4]{0,2,1:T(4,128)S(1)}, s32[48,2,4]{0,2,1:T(4,128)}, u32[]{:S(2)}) copy-start(s32[48,2,4]{0,2,1:T(4,128)} %param.5) | copy-start | bytes 4612
  56.5 1.2 copy-start.1
  57.7 1.1 copy-start.2
  81.2 2.0 %copy-start = (f32[768,1104]{1,0:T(8,128)S(1)}, f32[768,1104]{1,0:T(8,128)}, u32[]{:S(2)}) copy-start(f32[768,1104]{1,0:T(8,128)} %shard_map.47) | copy-start | bytes 10174468

commit v4 on v3

--- a/solution.py
+++ b/solution.py
@@ -106,16 +106,23 @@
                 device_id_type=mesh_id,
             )
         )
-        left_hops.append(
-            pltpu.make_async_remote_copy(
-                src_ref=left_ref,
-                dst_ref=left_out.at[me_col],
-                send_sem=left_send.at[d],
-                recv_sem=left_recv.at[d],
-                device_id={"col": other},
-                device_id_type=mesh_id,
-            )
+
+    paired = columns % 2 == 0
+    partner = me_col + 1 - 2 * lax.rem(me_col, 2)
+
+    def left_hop(i, source, slot, other):
+        return pltpu.make_async_remote_copy(
+            src_ref=source,
+            dst_ref=left_out.at[slot],
+            send_sem=left_send.at[i],
+            recv_sem=left_recv.at[i],
+            device_id={"col": other},
+            device_id_type=mesh_id,
         )
+
+    strides = range(2, columns, 2) if paired else range(1, columns)
+    left_hops = [left_hop(d, left_ref, me_col, lax.rem(me_col + d, columns)) for d in strides]
+    passed = [left_hop(1, left_ref, me_col, partner)] if paired else []
 
     def to_rows(d, source):
         slot = lax.rem(me_col + columns - d, columns)
@@ -134,16 +141,22 @@
     for hop in tile_hops:
         hop.start()
     to_rows(0, right_ref.at[me_col])
-    for hop in left_hops:
+    for hop in left_hops + passed:
         hop.start()
     left_out[me_col] = left_ref[...]
     right_out[me_row, me_col] = right_ref[me_col]
     for d, hop in enumerate(tile_hops, 1):
         hop.wait_recv()
         to_rows(d, right_out.at[me_row, lax.rem(me_col + columns - d, columns)])
-    for hop in left_hops + row_hops:
+    for d, hop in zip(strides, left_hops):
         hop.wait_recv()
-    for hop in tile_hops + left_hops + row_hops:
+        if paired:
+            slot = lax.rem(me_col + columns - d, columns)
+            passed.append(left_hop(d + 1, left_out.at[slot], slot, partner))
+            passed[-1].start()
+    for hop in passed + row_hops:
+        hop.wait_recv()
+    for hop in tile_hops + left_hops + passed + row_hops:
         hop.wait_send()
 
 

time: 146 us -> 139 us (0.952)
  Pallas kernels: 113 us -> 106 us
    pallas_call x1, Pallas kernels: 29.1 us -> 22.5 us  [gather(): pl.pallas_call(functools.partial(gather_kernel, columns, rows), in_specs=...]
where the time goes in v4:
time: 139 us
  Pallas kernels  106 us (76%)
  local copies, waits for them, and re-layouts  32.2 us (23%)
    pallas_call x1, Pallas kernels, ring_sum(): pl.pallas_call(functools.partial(ring_kernel, streams), in_specs=[whole],...  61.4 us
    pallas_call x1, Pallas kernels, gather(): pl.pallas_call(functools.partial(gather_kernel, columns, rows), in_specs=...  22.5 us
    pallas_call x1, Pallas kernels, product(): pl.pallas_call(functools.partial(product_kernel, pad), grid=(panels,), in...  22.4 us
    unnamed x14, local copies, waits for them, and re-layouts  13.2 us
    reshape x1, local copies, waits for them, and re-layouts, lay_right(): values.reshape(panels, rows, tiles, slots, edge, edge)  4.91 us
    reshape x1, local copies, waits for them, and re-layouts, lay_right(): blocks = blocks.reshape(tiles, panels, slots, edge, rows * (edge + 1))  4.3 us
    transpose x1, local copies, waits for them, and re-layouts, lay_left(): values.reshape(rows, panels, slots, edge, edge).transpose(1, 2, 4, 0, 3)  3.37 us

profile of v4, /device:TPU:0, one launch (start us, length us, event | category | flops | bytes accessed | tf_op | source)
XLA Modules:
  0.0 139.0 jit_solution(16092279467042511470)
XLA Ops:
  0.0 4.9 %reshape.29 = bf16[2,20,4,3,23,23]{5,4,2,3,1,0:T(8,128)(2,1)} reshape(bf16[2,20,4,3,529]{4,2,3,1,0:T(4,128)(2,1)} %param.6) | data formatting | bytes 1015680 | tf_op jit(solution)/shard_map/reshape | solution.py:26
  4.9 6.3 %copy.14 = bf16[4,2,3,23,20,23]{5,4,3,2,1,0:T(8,128)(2,1)S(1)} copy(bf16[4,2,3,23,20,23]{3,5,0,2,4,1:T(8,128)(2,1)} %bitcast.25) | data formatting | bytes 1015680
  11.2 2.5 %pad.4.clone = bf16[4,2,3,23,20,24]{5,4,3,2,1,0:T(8,128)(2,1)} pad(bf16[4,2,3,23,20,23]{5,4,3,2,1,0:T(8,128)(2,1)S(1)} %copy.14, bf16[]{:T(256)} %constant.2.clone.1), padding=0_0x0_0x0_0x0_0x0_0x0_1 | pad | bytes 1037762 | tf_op jit(solution)/shard_map/jit(_pad)/pad | solution.py:27
  13.7 4.3 %reshape.30 = bf16[4,2,3,23,480]{4,3,2,1,0:T(8,128)(2,1)S(1)} reshape(bf16[4,2,3,23,20,24]{5,4,3,2,1,0:T(8,128)(2,1)} %pad.4.clone) | data formatting | bytes 1059840 | tf_op jit(solution)/shard_map/reshape | solution.py:28
  18.0 0.0 copy-start.3
  18.0 0.1 broadcast_in_dim.7
  18.2 0.2 broadcast_in_dim_reshape.7
  18.4 0.2 pad_maximum_fusion.right_ref
  18.6 0.5 copy-done.3
  19.0 2.1 %copy.8 = bf16[48,2,4,529]{0,2,3,1:T(4,128)(2,1)} copy(bf16[48,2,4,529]{3,2,1,0:T(4,128)(2,1)S(1)} %copy-done.3) | data formatting | bytes 812544 | tf_op args[0]
  21.2 3.4 %copy.9 = bf16[2,4,23,48,23]{4,3,2,1,0:T(8,128)(2,1)S(1)} copy(bf16[2,4,23,48,23]{3,1,2,4,0:T(4,128)(2,1)} %bitcast.26) | data formatting | bytes 812544 | tf_op jit(solution)/shard_map/transpose | solution.py:17
  24.5 0.0 copy-start.5
  24.6 2.4 %reshape.28 = bf16[2,4,23,1104]{3,2,1,0:T(8,128)(2,1)S(1)} reshape(bf16[2,4,23,48,23]{4,3,2,1,0:T(8,128)(2,1)S(1)} %copy.9) | data formatting | bytes 812544 | tf_op jit(solution)/shard_map/reshape | solution.py:18
  27.0 0.1 broadcast_in_dim.6
  27.1 0.2 broadcast_in_dim_reshape.8
  27.3 0.1 pad_maximum_fusion.1.left_ref
  27.4 22.5 %shard_map.46 = (bf16[4,2,4,24,1104]{4,3,2,1,0:T(8,128)(2,1)S(1)}, bf16[2,4,2,3,24,480]{5,4,3,2,1,0:T(8,128)(2,1)S(1)}) custom-call(bf16[2,4,24,1104]{3,2,1,0:T(8,128)(2,1)S(1)} %pad_maximum_fusion.1.left_ref, bf16[4,2,3,24,480]{4,3,2,1,0:T(8,128)(2,1)S(1)} %pad_maximum_fusion.right_ref), custom_call_target="tpu_custom_call" | custom-call | tf_op jit(solution)/shard_map/pallas_call | solution.py:166
  49.9 1.2 copy-done.1
  51.1 1.1 copy-done.2
  52.1 22.4 %shard_map.47 = f32[768,1104]{1,0:T(8,128)} custom-call(bf16[8,4,24,1104]{3,2,1,0:T(8,128)(2,1)} %bitcast.23, bf16[2,8,3,24,480]{4,3,2,1,0:T(8,128)(2,1)} %bitcast.24), custom_call_target="tpu_custom_call" | custom-call | tf_op jit(solution)/shard_map/pallas_call | solution.py:72
  74.6 2.0 %copy-done = f32[768,1104]{1,0:T(8,128)S(1)} copy-done((f32[768,1104]{1,0:T(8,128)S(1)}, f32[768,1104]{1,0:T(8,128)}, u32[]{:S(2)}) %copy-start) | copy-done | bytes 3391512
  76.5 61.4 %shard_map.48 = f32[192,1104]{1,0:T(8,128)S(1)} custom-call(f32[4,192,1104]{2,1,0:T(8,128)S(1)} %bitcast.22), custom_call_target="tpu_custom_call" | custom-call | tf_op jit(solution)/shard_map/pallas_call | solution.py:226
  138.0 0.1 convert.4
  138.0 0.9 convert_element_type.25
  (10 shorter events, 0.1 us)
Async XLA Ops:
  13.7 4.3 %copy-start.4 = (s32[2,20,4,3]{1,2,3,0:T(4,128)S(1)}, s32[2,20,4,3]{1,2,3,0:T(4,128)}, u32[]{:S(2)}) copy-start(s32[2,20,4,3]{1,2,3,0:T(4,128)} %param.7) | copy-start | bytes 5764
  18.0 1.0 copy-start.3
  24.5 2.4 %copy-start.5 = (s32[48,2,4]{0,2,1:T(4,128)S(1)}, s32[48,2,4]{0,2,1:T(4,128)}, u32[]{:S(2)}) copy-start(s32[48,2,4]{0,2,1:T(4,128)} %param.5) | copy-start | bytes 4612
  49.9 1.2 copy-start.1
  51.1 1.1 copy-start.2
  74.5 2.0 %copy-start = (f32[768,1104]{1,0:T(8,128)S(1)}, f32[768,1104]{1,0:T(8,128)}, u32[]{:S(2)}) copy-start(f32[768,1104]{1,0:T(8,128)} %shard_map.47) | copy-start | bytes 10174468
